TPU v7x, 32 devices: a whole 2x2x4 slice. The times are simulated.
32 devices in a mesh: dx: 4 (over x, core), dy: 8 (over z, y).
Axes of the slice: x: 2, y: 2, z: 4, core: 2. Of those that a mesh axis runs over, the one named last changes fastest.
Arguments:
- positions: float32 [3, 65536], P(None, ('dx', 'dy')), may hold values from -6 to 6
- masses: float32 [65536], P(('dx', 'dy')), may hold values from 0.003 to 0.03
- centers: float32 [3, 32768], P(None, ('dx', 'dy')), may hold values from -3 to 3
- radii: float32 [32768], P(('dx', 'dy')), may hold values from 0.6 to 1.8
- pair_block: int32 [16384], P(('dx', 'dy')), may hold values from 0 to 15
- pair_halo: int32 [16384], P(('dx', 'dy')), may hold values from -1 to 1023, as said below
Outputs:
- centers_out: float32 [3, 32768], P(None, ('dx', 'dy'))
- radii_out: float32 [32768], P(('dx', 'dy'))
- profile: float32 [16, 32768], P(None, ('dx', 'dy'))
Inputs may be any that keep to these rules, and one draw needn't show every extreme that they name: `pair_halo`: for each domain and each owner, the 16 slots hold the live halo indices first and then -1; in every draw some owner receives 16 live slots from every domain.
All inputs are finite; a program needn't handle non-finite values.
Results may differ from a plain program's by a relative error of at most 0.0003.
Values sent between devices are 32-bit elements; how exact they have to be, the bound alone decides.
A program may use at most 64 MiB of HBM per device.

v0:
```python
import functools

import jax
import jax.numpy as jnp
from jax import lax
from jax.experimental import pallas as pl
from jax.experimental.pallas import tpu as pltpu
from jax.sharding import PartitionSpec as P

SHELLS = 16
BLOCK = 128
ITERS = 2
GROUP = 8
ROWS = 32
CHUNK = 32


def split3(value):
    high = value.astype(jnp.bfloat16)
    rest = value - high.astype(jnp.float32)
    middle = rest.astype(jnp.bfloat16)
    low = (rest - middle.astype(jnp.float32)).astype(jnp.bfloat16)
    return jnp.concatenate([high, middle, low], axis=0)


def join3(value):
    rows = value.shape[0] // 3
    return value[:rows] + (value[rows : 2 * rows] + value[2 * rows :])


def kernel(
    sizes,
    pos, mass, cen, rad, blocks, halos,
    cen_out, rad_out, prof_out,
    raw_pos, raw_mass, raw_pair, data, pick, points, onehot, terms, state, asked,
    local_sem, send_sem, recv_sem, fwd_send,
):
    ndx, ndy, slots, count = sizes
    n = ndx * ndy
    half = n // 2
    groups = n // GROUP
    halo_dev = rad.shape[1]
    mx = lax.axis_index("dx")
    my = lax.axis_index("dy")
    me = mx * ndy + my
    core = lax.rem(mx, 2)
    sib = mx + 1 - 2 * core
    size_a, size_b, size_c = ndx // 2, 2, ndy // 2
    size2 = size_b if size_a == size_b else size_b + core * (size_a - size_b)
    size3 = size_a if size_a == size_b else size_a + core * (size_b - size_a)
    plane = size2 * size_c
    MESH = pl.DeviceIdType.MESH

    def shifted(step3, step2, step1):
        step_a = (1 - core) * step3 + core * step2
        step_b = (1 - core) * step2 + core * step3
        tx = lax.rem(mx + 2 * step_a, ndx)
        ty = lax.rem(my // 2 + step1, size_c) * 2 + lax.rem(lax.rem(my, 2) + step_b, 2)
        return tx, ty

    def each(low, high, act):
        if isinstance(high, int):
            for i in range(low, high):
                act(i)
        else:

            def one(i, _):
                act(i)
                return 0

            lax.fori_loop(low, high, one, 0)

    def when(known, act):
        if isinstance(known, bool):
            if known:
                act()
        else:
            pl.when(known)(act)

    def send(source, slot, device):
        return pltpu.make_async_remote_copy(
            src_ref=data.at[source], dst_ref=data.at[slot],
            send_sem=send_sem.at[slot], recv_sem=recv_sem.at[slot],
            device_id=device, device_id_type=MESH,
        )

    def forward(t):
        return pltpu.make_async_remote_copy(
            src_ref=data.at[t], dst_ref=data.at[half + t],
            send_sem=fwd_send.at[t], recv_sem=recv_sem.at[half + t],
            device_id=(sib, my), device_id_type=MESH,
        )

    def send_line(q):
        each(1, size_c, lambda i: send(q, q + i, shifted(0, 0, i)).start())

    def send_second(q):
        each(1, size2, lambda i: send(q, q + i * size_c, shifted(0, i, 0)).start())

    def send_third(q):
        each(1, size3, lambda i: send(q, q + i * plane, shifted(i, 0, 0)).start())

    def relay(q):
        when(q < plane, lambda: send_third(q))
        when(q < size_c, lambda: send_second(q))
        forward(q).start()

    row_me = (me * slots) // 128
    own = [
        pltpu.make_async_copy(pos, raw_pos, local_sem.at[0]),
        pltpu.make_async_copy(mass, raw_mass, local_sem.at[1]),
        pltpu.make_async_copy(blocks, raw_pair.at[0], local_sem.at[2]),
        pltpu.make_async_copy(halos, raw_pair.at[1], local_sem.at[3]),
        pltpu.make_async_copy(cen, cen_out, local_sem.at[4]),
        pltpu.make_async_copy(rad, rad_out, local_sem.at[5]),
    ]
    barrier = pltpu.get_barrier_semaphore()

    def greet(device):
        pl.semaphore_signal(barrier, inc=1, device_id=device, device_id_type=MESH)

    greet((sib, my))
    each(1, size_c, lambda i: greet(shifted(0, 0, i)))
    each(1, size2, lambda i: greet(shifted(0, i, 0)))
    each(1, size3, lambda i: greet(shifted(i, 0, 0)))
    for copy in own:
        copy.start()
    for copy in own:
        copy.wait()
    for b in range(count):
        part = raw_pos[:, b * BLOCK : (b + 1) * BLOCK]
        for i in range(3):
            data[0, i * count + b : i * count + b + 1, :] = part[i : i + 1]
    data[0, 3 * count : 4 * count, :] = raw_mass[...]
    pair_rows = raw_pair.shape[1]
    for i in range(2):
        at = 4 * count + i * pair_rows
        data[0, at : at + pair_rows, :] = raw_pair[i].astype(jnp.float32)
    state[...] = jnp.zeros_like(state)
    terms[...] = jnp.zeros_like(terms)
    state[0:3, :] = cen_out[...]
    state[3:4, :] = rad_out[...]
    pl.semaphore_wait(barrier, size_a + size_b + size_c - 2)

    send_line(0)
    relay(0)

    lane0 = me * slots - row_me * 128
    lanes = lax.broadcasted_iota(jnp.int32, (GROUP, halo_dev), 1).astype(jnp.float32)
    spots = lax.broadcasted_iota(jnp.int32, (GROUP, GROUP * count), 1).astype(jnp.float32)
    place = lax.broadcasted_iota(jnp.int32, (GROUP, 128), 0).astype(jnp.float32)
    shift = lax.rem(128 - lane0, 128)

    def prepare(g):
        lo = g * GROUP * slots
        if not isinstance(g, int):
            lo = pl.multiple_of(lo, GROUP * slots)

        def taken(i):
            at = 4 * count + i * pair_rows + row_me
            part = data[pl.ds(g * GROUP, GROUP), pl.ds(at, 1), :].reshape(GROUP, 128)
            return pltpu.roll(part, shift, 1)

        rows = taken(1)
        want = taken(0) + place * float(count)
        for j in range(0, slots, 2):
            start = lo + j * GROUP
            for values, iota, out in ((rows, lanes, onehot), (want, spots, pick)):
                pair = [
                    jnp.where(values[:, i : i + 1] == iota, 1.0, 0.0) for i in (j, j + 1)
                ]
                both = jnp.concatenate(pair, axis=0).astype(jnp.bfloat16)
                out[pl.ds(start, 2 * GROUP), :] = both
        asked[:, pl.ds(lo, GROUP * slots)] = join3(
            lax.dot_general(
                split3(state[...]), onehot[pl.ds(lo, GROUP * slots), :], (((1,), (1,)), ((), ())),
                preferred_element_type=jnp.float32,
            )
        )

    def ask():
        asked[...] = join3(
            lax.dot_general(
                split3(state[...]), onehot[...], (((1,), (1,)), ((), ())),
                preferred_element_type=jnp.float32,
            )
        )

    width = GROUP * slots

    def evaluate(g):
        lo = pl.multiple_of(g * width, width)
        mine = asked[0:4, pl.ds(lo, width)]
        cx, cy, cz, radius = (mine[i : i + 1] for i in range(4))
        scale = (SHELLS / 2.0) / jnp.where(radius > 0.0, radius, 1.0)

        def fold(value):
            return jnp.sum(value.reshape(CHUNK // 8, 8, width), axis=0)

        def chunk(c, acc):
            at = pl.ds(pl.multiple_of(c * CHUNK, CHUNK), CHUNK)
            ox = points[g, 0, at] - cx
            oy = points[g, 1, at] - cy
            oz = points[g, 2, at] - cz
            m = points[g, 3, at]
            u = jnp.sqrt(ox * ox + oy * oy + oz * oz) * scale
            top = m * jnp.minimum(u + 0.5, 1.0)
            ramp = m * (1.5 - u)
            out = []
            for k in range(SHELLS):
                out.append(acc[k] + fold(jnp.maximum(jnp.minimum(top, ramp), 0.0)))
                ramp = ramp + m
            inner = m * jnp.clip(SHELLS / 2.0 - u, 0.0, 1.0)
            out.append(acc[SHELLS] + fold(inner))
            for i, o in enumerate((ox, oy, oz)):
                out.append(acc[SHELLS + 1 + i] + fold(o * inner))
            return tuple(out)

        zero = jnp.zeros((8, width), jnp.float32)
        acc = lax.fori_loop(0, BLOCK // CHUNK, chunk, (zero,) * (SHELLS + 4))
        for k in range(SHELLS + 4):
            terms[k : k + 1, pl.ds(lo, width)] = jnp.sum(acc[k], axis=0, keepdims=True)

    def choose(g):
        chosen = pick[pl.ds(pl.multiple_of(g * width, width), width), :]
        for i in range(4):
            flat = data[pl.ds(g * GROUP, GROUP), i * count : (i + 1) * count, :]
            flat = flat.reshape(GROUP * count, BLOCK).T
            points[g, i] = join3(
                lax.dot_general(
                    split3(flat), chosen, (((1,), (1,)), ((), ())),
                    preferred_element_type=jnp.float32,
                )
            )

    def arrive(q):
        send(0, q, (sib, my)).wait_recv()
        relay(q)

    def compute(g):
        prepare(g)
        choose(g)
        evaluate(g)

    def late(g, _):
        for i in range(GROUP):
            send(0, g * GROUP + i, (sib, my)).wait_recv()
        compute(g)
        return 0

    def again(g, _):
        evaluate(g)
        return 0

    def advance():
        sums = join3(
            lax.dot_general(
                split3(terms[...]), onehot[...], (((1,), (0,)), ((), ())),
                preferred_element_type=jnp.float32,
            )
        )
        radius = state[3:4, :]
        enclosed = sums[SHELLS // 2 - 1 : SHELLS // 2]
        ratio = (1.0 + enclosed) / (1.0 + radius * radius * radius)
        state[3:4, :] = radius * jnp.exp(jnp.log(ratio) * (1.0 / 3.0))
        total = jnp.maximum(sums[SHELLS : SHELLS + 1], 1.0)
        state[0:3, :] = state[0:3, :] + sums[SHELLS + 1 : SHELLS + 4] / total
        return sums

    def delay(q):
        if not isinstance(plane, int):
            return q
        step1 = q % size_c
        hops = min(step1, size_c - step1)
        stages = (step1 > 0) + (q // size_c % size2 > 0) + (q // plane > 0)
        return hops + 2 * stages

    order = sorted(range(1, half), key=delay)
    if isinstance(plane, int) and plane <= GROUP:
        order = [q for q in order if q < GROUP or delay(q) <= 4] + [
            q for q in order if q >= GROUP and delay(q) > 4
        ]
    done = {0}
    g = 0
    for q in order:
        arrive(q)
        done.add(q)
        while g < groups // 2 and done.issuperset(range(g * GROUP, (g + 1) * GROUP)):
            compute(g)
            g += 1
    lax.fori_loop(groups // 2, groups, late, 0)
    sums = advance()
    for step in range(1, ITERS):
        ask()
        lax.fori_loop(0, groups, again, 0)
        sums = advance()
    cen_out[...] = state[0:3, :]
    rad_out[...] = state[3:4, :]
    prof_out[...] = sums[:SHELLS]

    def finish(t, _):
        @pl.when(t > 0)
        def _():
            send(0, t, (sib, my)).wait_send()

        forward(t).wait_send()
        return 0

    lax.fori_loop(0, half, finish, 0)


def hand(a, b, c, x, y, z):
    x[...] = a[...]
    y[...] = b[...]
    z[...] = c[...]


def body(positions, masses, centers, radii, pair_block, pair_halo):
    ndx = lax.axis_size("dx")
    ndy = lax.axis_size("dy")
    n = ndx * ndy
    halo_dev = radii.shape[0]
    count = masses.shape[0] // BLOCK
    slots = pair_halo.shape[0] // n
    total = n * slots
    groups = n // GROUP
    any_ref = pl.BlockSpec(memory_space=pl.ANY)
    vmem = pl.BlockSpec(memory_space=pltpu.VMEM)
    f32 = jnp.float32
    dma = pltpu.SemaphoreType.DMA
    out = pl.pallas_call(
        functools.partial(kernel, (ndx, ndy, slots, count)),
        out_shape=(
            jax.ShapeDtypeStruct((3, halo_dev), f32),
            jax.ShapeDtypeStruct((1, halo_dev), f32),
            jax.ShapeDtypeStruct((SHELLS, halo_dev), f32),
        ),
        in_specs=[any_ref] * 6,
        out_specs=(vmem,) * 3,
        scratch_shapes=[
            pltpu.VMEM((3, count * BLOCK), f32),
            pltpu.VMEM((count, BLOCK), f32),
            pltpu.VMEM((2, total // 128, 128), jnp.int32),
            pltpu.VMEM((n, 4 * count + 2 * (total // 128), BLOCK), f32),
            pltpu.VMEM((total, GROUP * count), jnp.bfloat16),
            pltpu.VMEM((groups, 4, BLOCK, GROUP * slots), f32),
            pltpu.VMEM((total, halo_dev), jnp.bfloat16),
            pltpu.VMEM((ROWS, total), f32),
            pltpu.VMEM((16, halo_dev), f32),
            pltpu.VMEM((16, total), f32),
            dma((6,)),
            dma((n // 2,)),
            dma((n,)),
            dma((n // 2,)),
        ],
        compiler_params=pltpu.CompilerParams(collective_id=0, has_side_effects=True),
    )(
        positions,
        masses.reshape(count, BLOCK),
        centers,
        radii.reshape(1, halo_dev),
        pair_block.reshape(total // 128, 128),
        pair_halo.reshape(total // 128, 128),
    )
    out = pl.pallas_call(
        hand,
        out_shape=tuple(jax.ShapeDtypeStruct(x.shape, f32) for x in out),
        in_specs=[vmem] * 3,
        out_specs=(vmem,) * 3,
    )(*out)
    return out[0], out[1].reshape(halo_dev), out[2]


def solution(mesh):
    flat = P(("dx", "dy"))
    rows = P(None, ("dx", "dy"))
    in_specs = (rows, flat, rows, flat, flat, flat)
    out_specs = (rows, flat, rows)
    return jax.shard_map(body, mesh=mesh, in_specs=in_specs, out_specs=out_specs, check_vma=False)
```

profile of v0, /device:TPU:0, one launch (start us, length us, event | category | flops | bytes accessed | tf_op | source)
XLA Modules:
  0.0 25.0 jit_solution(16616429293760602647)
XLA Ops:
  0.6 22.9 %shard_map.85 = (f32[3,1024]{1,0:T(4,128)}, f32[1,1024]{1,0:T(1,128)}, f32[16,1024]{1,0:T(8,128)}) custom-call(f32[3,2048]{1,0:T(4,128)} %pos.1, f32[16,128]{1,0:T(8,128)} %bitcast.5, f32[3,1024]{1,0:T(4,128)} %cen.1, f32[1,1024]{1,0:T(1,128)} %bitcast.6, s32[4,128]{1,0:T(4,128)} %bitcast.7, s32[4,128]{1,0:T(4,128)} %bitcast.8), custom_call_target="tpu_custom_call" | custom-call | tf_op jit(solution)/shard_map/pallas_call | solution.py:331
  23.5 1.5 %shard_map.86 = (f32[3,1024]{1,0:T(4,128)}, f32[1,1024]{1,0:T(1,128)}, f32[16,1024]{1,0:T(8,128)}) custom-call(f32[3,1024]{1,0:T(4,128)} %get-tuple-element.9.a, f32[1,1024]{1,0:T(1,128)} %get-tuple-element.10.b, f32[16,1024]{1,0:T(8,128)} %get-tuple-element.11.c), custom_call_target="tpu_custom_call" | custom-call | tf_op jit(solution)/shard_map/pallas_call | solution.py:365
where the time goes:
time: 25.3 us; the launch traced here: 25 us
  Pallas kernels  24.4 us (96%)
  between operations  0.64 us (3%)
    pallas_call x1, Pallas kernels, body(): pl.pallas_call(functools.partial(kernel, (ndx, ndy, slots, count)), out_s...  22.9 us
    pallas_call x1, Pallas kernels, body(): pl.pallas_call(hand, out_shape=tuple((jax.ShapeDtypeStruct(x.shape, f32)...  1.5 us

commit v1 on v0

--- a/solution.py
+++ b/solution.py
@@ -13,6 +13,7 @@
 GROUP = 8
 ROWS = 32
 CHUNK = 32
+HUB = 0
 
 
 def split3(value):
@@ -33,7 +34,7 @@
     pos, mass, cen, rad, blocks, halos,
     cen_out, rad_out, prof_out,
     raw_pos, raw_mass, raw_pair, data, pick, points, onehot, terms, state, asked,
-    local_sem, send_sem, recv_sem, fwd_send,
+    local_sem, send_sem, recv_sem, ready,
 ):
     ndx, ndy, slots, count = sizes
     n = ndx * ndy
@@ -44,68 +45,135 @@
     my = lax.axis_index("dy")
     me = mx * ndy + my
     core = lax.rem(mx, 2)
-    sib = mx + 1 - 2 * core
     size_a, size_b, size_c = ndx // 2, 2, ndy // 2
-    size2 = size_b if size_a == size_b else size_b + core * (size_a - size_b)
-    size3 = size_a if size_a == size_b else size_a + core * (size_b - size_a)
-    plane = size2 * size_c
     MESH = pl.DeviceIdType.MESH
 
-    def shifted(step3, step2, step1):
-        step_a = (1 - core) * step3 + core * step2
-        step_b = (1 - core) * step2 + core * step3
-        tx = lax.rem(mx + 2 * step_a, ndx)
-        ty = lax.rem(my // 2 + step1, size_c) * 2 + lax.rem(lax.rem(my, 2) + step_b, 2)
-        return tx, ty
-
-    def each(low, high, act):
-        if isinstance(high, int):
-            for i in range(low, high):
-                act(i)
+    def flip(value, step, size):
+        if size & (size - 1):
+            return lax.rem(value + step, size)
+        bit = 1
+        while bit < size:
+            if step & bit:
+                value = value + bit * (1 - 2 * lax.rem(value // bit, 2))
+            bit *= 2
+        return value
+
+    def at_step(step3, step2, step1):
+        a, b, c = mx // 2, lax.rem(my, 2), my // 2
+        c = flip(c, step1, size_c)
+        if size_a == size_b:
+            a0, b0 = flip(a, step3, size_a), flip(b, step2, size_b)
+            a1, b1 = flip(a, step2, size_a), flip(b, step3, size_b)
+            a, b = a0 + core * (a1 - a0), b0 + core * (b1 - b0)
         else:
-
-            def one(i, _):
-                act(i)
-                return 0
-
-            lax.fori_loop(low, high, one, 0)
-
-    def when(known, act):
-        if isinstance(known, bool):
-            if known:
-                act()
-        else:
-            pl.when(known)(act)
-
-    def send(source, slot, device):
+            a, b = flip(a, step3, size_a), flip(b, step2, size_b)
+        return 2 * a + core, 2 * c + b
+
+    sibling = (mx + 1 - 2 * core, my)
+    row_me = (me * slots) // 128
+    pair_rows = raw_pair.shape[1]
+
+    def label(p3, p2, p1):
+        return (p3 * size_b + p2) * size_c + p1
+
+    line = list(range(size_c))
+    plane = [(p3, p2) for p3 in range(size_a) for p2 in range(size_b) if p3 or p2]
+    plane.sort(key=lambda p: -(p[0] > 0) - (p[1] > 0))
+
+    rank = []
+    for p1 in line:
+        rank.append((0, p1, 0, label(0, 0, p1)))
+        rank.append((0, p1, 1, label(0, 0, p1) + half))
+        for p3, p2 in plane:
+            rank.append((1, p1, 0, label(p3, p2, p1)))
+            rank.append((1, p1, 1, label(p3, p2, p1) + half))
+    rank.sort()
+    place_of = {t: i for i, (_, _, _, t) in enumerate(rank)}
+
+    kinds = (None, data)
+    first = jnp.logical_and(mx // 2 == 0, my == 0)
+    hub = half <= HUB
+
+    def coords(p3, p2):
+        if size_a == size_b:
+            return p3 + core * (p2 - p3), p2 + core * (p3 - p2)
+        return p3, p2
+
+    def inward(p3, p2, p1):
+        a, b = coords(p3, p2)
+        far = (mx // 2 - a) * (mx // 2 - a) + (lax.rem(my, 2) - b) * (lax.rem(my, 2) - b)
+        return far + (my // 2 - p1) * (my // 2 - p1) == 0
+
+    def copy(kind, source, target, device):
+        u = kind * n
         return pltpu.make_async_remote_copy(
-            src_ref=data.at[source], dst_ref=data.at[slot],
-            send_sem=send_sem.at[slot], recv_sem=recv_sem.at[slot],
+            src_ref=kinds[kind].at[place_of[source]], dst_ref=kinds[kind].at[place_of[target]],
+            send_sem=send_sem.at[u + target], recv_sem=recv_sem.at[u + target],
             device_id=device, device_id_type=MESH,
         )
 
-    def forward(t):
-        return pltpu.make_async_remote_copy(
-            src_ref=data.at[t], dst_ref=data.at[half + t],
-            send_sem=fwd_send.at[t], recv_sem=recv_sem.at[half + t],
-            device_id=(sib, my), device_id_type=MESH,
-        )
-
-    def send_line(q):
-        each(1, size_c, lambda i: send(q, q + i, shifted(0, 0, i)).start())
-
-    def send_second(q):
-        each(1, size2, lambda i: send(q, q + i * size_c, shifted(0, i, 0)).start())
-
-    def send_third(q):
-        each(1, size3, lambda i: send(q, q + i * plane, shifted(i, 0, 0)).start())
-
-    def relay(q):
-        when(q < plane, lambda: send_third(q))
-        when(q < size_c, lambda: send_second(q))
-        forward(q).start()
-
-    row_me = (me * slots) // 128
+    sent = []
+
+    def launch(kind, source, target, device, go=None):
+        one = copy(kind, source, target, device)
+        if go is None:
+            one.start()
+        else:
+            pl.when(go)(one.start)
+        sent.append((one, go))
+
+    zed = my // 2
+    spot = (mx // 2) * size_b + lax.rem(my, 2)
+
+    def outer_line(step):
+        return flip(zed, step, size_c) > zed
+
+    def outer_plane(p3, p2):
+        tx, ty = at_step(p3, p2, 0)
+        return (tx // 2) * size_b + lax.rem(ty, 2) > spot
+
+    peers = [(0, 0, step) for step in line[1:]] + [(p3, p2, 0) for p3, p2 in plane]
+    peers.sort(key=lambda p: (p[0] > 0) + (p[1] > 0) + p[2])
+
+    def outer(peer):
+        return outer_line(peer[2]) if peer[2] else outer_plane(peer[0], peer[1])
+
+    def relay(kind, t):
+        p1 = t % size_c
+        if 0 < t < size_c:
+            for p3, p2 in plane:
+                go = jnp.logical_not(inward(p3, p2, 0)) if hub else None
+                launch(kind, t, label(p3, p2, p1), at_step(p3, p2, 0), go)
+        if t < half:
+            launch(kind, t, t + half, sibling)
+
+    def begin(kind):
+        if hub:
+            for p3, p2 in plane:
+                for step in line[1:]:
+                    launch(kind, 0, label(p3, p2, step), at_step(p3, p2, step), inward(p3, p2, step))
+        for peer in reversed(peers):
+            go = jnp.logical_not(outer(peer))
+            launch(kind, 0, label(*peer), at_step(*peer), go)
+
+        @pl.when(core == 0)
+        def _():
+            pl.semaphore_wait(ready.at[0], 1)
+
+        relay(kind, 0)
+        for peer in peers:
+            go = outer(peer)
+
+            @pl.when(go)
+            def _(peer=peer):
+                pl.semaphore_wait(ready.at[label(*peer)], 1)
+
+            launch(kind, 0, label(*peer), at_step(*peer), go)
+
+    def arrive(kind, t):
+        copy(kind, 0, t, sibling).wait_recv()
+        relay(kind, t)
+
     own = [
         pltpu.make_async_copy(pos, raw_pos, local_sem.at[0]),
         pltpu.make_async_copy(mass, raw_mass, local_sem.at[1]),
@@ -119,31 +187,50 @@
     def greet(device):
         pl.semaphore_signal(barrier, inc=1, device_id=device, device_id_type=MESH)
 
-    greet((sib, my))
-    each(1, size_c, lambda i: greet(shifted(0, 0, i)))
-    each(1, size2, lambda i: greet(shifted(0, i, 0)))
-    each(1, size3, lambda i: greet(shifted(i, 0, 0)))
-    for copy in own:
-        copy.start()
-    for copy in own:
-        copy.wait()
+    def answer(t, device):
+        pl.semaphore_signal(ready.at[t], inc=1, device_id=device, device_id_type=MESH)
+
+    for one in own:
+        one.start()
+    for peer in peers:
+        pl.when(outer(peer))(functools.partial(greet, at_step(*peer)))
+    pl.when(core == 0)(functools.partial(greet, sibling))
+    extra = 0
+    if hub:
+
+        @pl.when(first)
+        def _():
+            for p3, p2 in plane:
+                for step in line[1:]:
+                    greet(at_step(p3, p2, step))
+
+        off = jnp.minimum(spot, 1)
+        extra = off * jnp.minimum(zed, 1)
+    lower = zed + spot + core + extra
+
+    @pl.when(lower > 0)
+    def _():
+        pl.semaphore_wait(barrier, lower)
+
+    for peer in peers:
+        pl.when(jnp.logical_not(outer(peer)))(functools.partial(answer, label(*peer), at_step(*peer)))
+    pl.when(core == 1)(functools.partial(answer, 0, sibling))
+    for one in own:
+        one.wait()
+    mine = place_of[0]
     for b in range(count):
         part = raw_pos[:, b * BLOCK : (b + 1) * BLOCK]
         for i in range(3):
-            data[0, i * count + b : i * count + b + 1, :] = part[i : i + 1]
-    data[0, 3 * count : 4 * count, :] = raw_mass[...]
-    pair_rows = raw_pair.shape[1]
+            data[mine, i * count + b : i * count + b + 1, :] = part[i : i + 1]
+    data[mine, 3 * count : 4 * count, :] = raw_mass[...]
     for i in range(2):
         at = 4 * count + i * pair_rows
-        data[0, at : at + pair_rows, :] = raw_pair[i].astype(jnp.float32)
+        data[mine, at : at + pair_rows, :] = raw_pair[i].astype(jnp.float32)
     state[...] = jnp.zeros_like(state)
     terms[...] = jnp.zeros_like(terms)
     state[0:3, :] = cen_out[...]
     state[3:4, :] = rad_out[...]
-    pl.semaphore_wait(barrier, size_a + size_b + size_c - 2)
-
-    send_line(0)
-    relay(0)
+    begin(1)
 
     lane0 = me * slots - row_me * 128
     lanes = lax.broadcasted_iota(jnp.int32, (GROUP, halo_dev), 1).astype(jnp.float32)
@@ -233,20 +320,9 @@
                 )
             )
 
-    def arrive(q):
-        send(0, q, (sib, my)).wait_recv()
-        relay(q)
-
     def compute(g):
-        prepare(g)
         choose(g)
         evaluate(g)
-
-    def late(g, _):
-        for i in range(GROUP):
-            send(0, g * GROUP + i, (sib, my)).wait_recv()
-        compute(g)
-        return 0
 
     def again(g, _):
         evaluate(g)
@@ -267,28 +343,30 @@
         state[0:3, :] = state[0:3, :] + sums[SHELLS + 1 : SHELLS + 4] / total
         return sums
 
-    def delay(q):
-        if not isinstance(plane, int):
-            return q
-        step1 = q % size_c
-        hops = min(step1, size_c - step1)
-        stages = (step1 > 0) + (q // size_c % size2 > 0) + (q // plane > 0)
-        return hops + 2 * stages
-
-    order = sorted(range(1, half), key=delay)
-    if isinstance(plane, int) and plane <= GROUP:
-        order = [q for q in order if q < GROUP or delay(q) <= 4] + [
-            q for q in order if q >= GROUP and delay(q) > 4
-        ]
-    done = {0}
-    g = 0
-    for q in order:
-        arrive(q)
-        done.add(q)
-        while g < groups // 2 and done.issuperset(range(g * GROUP, (g + 1) * GROUP)):
-            compute(g)
-            g += 1
-    lax.fori_loop(groups // 2, groups, late, 0)
+    split = kinds[0] is not None
+
+    def both(t):
+        if split:
+            arrive(0, t)
+        arrive(1, t)
+
+    if split:
+        for t in line[1:]:
+            arrive(0, t)
+    for t in line[1:]:
+        arrive(1, t)
+    level = [rank[i][1] if rank[i][0] else -1 for i in range(n)]
+    done = 0
+    for p1 in line:
+        for p3, p2 in reversed(plane):
+            both(label(p3, p2, p1))
+        while done < groups and (p1 == line[-1] or level[(done + 1) * GROUP - 1] < p1):
+            for i in range(done * GROUP, (done + 1) * GROUP):
+                if rank[i][3] >= half:
+                    both(rank[i][3])
+            prepare(done)
+            compute(done)
+            done += 1
     sums = advance()
     for step in range(1, ITERS):
         ask()
@@ -297,22 +375,22 @@
     cen_out[...] = state[0:3, :]
     rad_out[...] = state[3:4, :]
     prof_out[...] = sums[:SHELLS]
-
-    def finish(t, _):
-        @pl.when(t > 0)
-        def _():
-            send(0, t, (sib, my)).wait_send()
-
-        forward(t).wait_send()
-        return 0
-
-    lax.fori_loop(0, half, finish, 0)
-
-
-def hand(a, b, c, x, y, z):
-    x[...] = a[...]
-    y[...] = b[...]
-    z[...] = c[...]
+    for one, go in sent:
+        if go is None:
+            one.wait_send()
+        else:
+            pl.when(go)(one.wait_send)
+
+
+def hand(a, b, c, x, y, z, sem):
+    copies = [
+        pltpu.make_async_copy(source, target, sem.at[i])
+        for i, (source, target) in enumerate(((a, x), (b, y), (c, z)))
+    ]
+    for copy in copies:
+        copy.start()
+    for copy in copies:
+        copy.wait()
 
 
 def body(positions, masses, centers, radii, pair_block, pair_halo):
@@ -331,9 +409,9 @@
     out = pl.pallas_call(
         functools.partial(kernel, (ndx, ndy, slots, count)),
         out_shape=(
-            jax.ShapeDtypeStruct((3, halo_dev), f32),
-            jax.ShapeDtypeStruct((1, halo_dev), f32),
-            jax.ShapeDtypeStruct((SHELLS, halo_dev), f32),
+            pltpu.VMEM((3, halo_dev), f32),
+            pltpu.VMEM((1, halo_dev), f32),
+            pltpu.VMEM((SHELLS, halo_dev), f32),
         ),
         in_specs=[any_ref] * 6,
         out_specs=(vmem,) * 3,
@@ -349,9 +427,9 @@
             pltpu.VMEM((16, halo_dev), f32),
             pltpu.VMEM((16, total), f32),
             dma((6,)),
-            dma((n // 2,)),
-            dma((n,)),
-            dma((n // 2,)),
+            dma((2 * n,)),
+            dma((2 * n,)),
+            pltpu.SemaphoreType.REGULAR((n // 2,)),
         ],
         compiler_params=pltpu.CompilerParams(collective_id=0, has_side_effects=True),
     )(
@@ -362,11 +440,13 @@
         pair_block.reshape(total // 128, 128),
         pair_halo.reshape(total // 128, 128),
     )
+    out = [pltpu.with_memory_space_constraint(x, pltpu.VMEM) for x in out]
     out = pl.pallas_call(
         hand,
         out_shape=tuple(jax.ShapeDtypeStruct(x.shape, f32) for x in out),
         in_specs=[vmem] * 3,
-        out_specs=(vmem,) * 3,
+        out_specs=(any_ref,) * 3,
+        scratch_shapes=[dma((3,))],
     )(*out)
     return out[0], out[1].reshape(halo_dev), out[2]
 

time: 25.3 us -> 20.8 us (0.82)
  Pallas kernels: 24.4 us -> 19.9 us
    pallas_call x1, Pallas kernels: 22.9 us -> 19.3 us  [body(): pl.pallas_call(functools.partial(kernel, (ndx, ndy, slots, count)), out_s...]
    pallas_call x1, Pallas kernels: 1.5 us -> 0.67 us  [body(): pl.pallas_call(hand, out_shape=tuple((jax.ShapeDtypeStruct(x.shape, f32)...]
where the time goes in v1:
time: 20.8 us; the launch traced here: 20.6 us
  Pallas kernels  19.9 us (96%)
  between operations  0.64 us (3%)
    pallas_call x1, Pallas kernels, body(): pl.pallas_call(functools.partial(kernel, (ndx, ndy, slots, count)), out_s...  19.3 us
    pallas_call x1, Pallas kernels, body(): pl.pallas_call(hand, out_shape=tuple((jax.ShapeDtypeStruct(x.shape, f32)...  0.67 us

profile of v1, /device:TPU:0, one launch (start us, length us, event | category | flops | bytes accessed | tf_op | source)
XLA Modules:
  0.0 20.6 jit_solution(16326499055365066764)
XLA Ops:
  0.6 19.3 %shard_map.85 = (f32[3,1024]{1,0:T(4,128)S(1)}, f32[1,1024]{1,0:T(1,128)S(1)}, f32[16,1024]{1,0:T(8,128)S(1)}) custom-call(f32[3,2048]{1,0:T(4,128)} %pos.1, f32[16,128]{1,0:T(8,128)} %bitcast.5, f32[3,1024]{1,0:T(4,128)} %cen.1, f32[1,1024]{1,0:T(1,128)} %bitcast.6, s32[4,128]{1,0:T(4,128)} %bitcast.7, s32[4,128]{1,0:T(4,128)} %bitcast.8), custom_call_target="tpu_custom_call" | custom-call | tf_op jit(solution)/shard_map/pallas_call | solution.py:409
  19.9 0.7 %shard_map.86 = (f32[3,1024]{1,0:T(4,128)}, f32[1,1024]{1,0:T(1,128)}, f32[16,1024]{1,0:T(8,128)}) custom-call(f32[3,1024]{1,0:T(4,128)S(1)} %get-tuple-element.9.a, f32[1,1024]{1,0:T(1,128)S(1)} %get-tuple-element.10.b, f32[16,1024]{1,0:T(8,128)S(1)} %get-tuple-element.11.c), custom_call_target="tpu_custom_call" | custom-call | tf_op jit(solution)/shard_map/pallas_call | solution.py:444

commit v2 on v1

--- a/solution.py
+++ b/solution.py
@@ -13,7 +13,7 @@
 GROUP = 8
 ROWS = 32
 CHUNK = 32
-HUB = 0
+SMALL = 4
 
 
 def split3(value):
@@ -90,37 +90,22 @@
     rank.sort()
     place_of = {t: i for i, (_, _, _, t) in enumerate(rank)}
 
-    kinds = (None, data)
-    first = jnp.logical_and(mx // 2 == 0, my == 0)
-    hub = half <= HUB
-
-    def coords(p3, p2):
-        if size_a == size_b:
-            return p3 + core * (p2 - p3), p2 + core * (p3 - p2)
-        return p3, p2
-
-    def inward(p3, p2, p1):
-        a, b = coords(p3, p2)
-        far = (mx // 2 - a) * (mx // 2 - a) + (lax.rem(my, 2) - b) * (lax.rem(my, 2) - b)
-        return far + (my // 2 - p1) * (my // 2 - p1) == 0
-
-    def copy(kind, source, target, device):
-        u = kind * n
+    def lane_of(t):
+        return t - 1 if t < half else half - 1 + place_of[t] // GROUP
+
+    def copy(source, target, device):
         return pltpu.make_async_remote_copy(
-            src_ref=kinds[kind].at[place_of[source]], dst_ref=kinds[kind].at[place_of[target]],
-            send_sem=send_sem.at[u + target], recv_sem=recv_sem.at[u + target],
+            src_ref=data.at[place_of[source]], dst_ref=data.at[place_of[target]],
+            send_sem=send_sem.at[0], recv_sem=recv_sem.at[lane_of(target)],
             device_id=device, device_id_type=MESH,
         )
 
-    sent = []
-
-    def launch(kind, source, target, device, go=None):
-        one = copy(kind, source, target, device)
-        if go is None:
-            one.start()
-        else:
-            pl.when(go)(one.start)
-        sent.append((one, go))
+    def several(size, lane):
+        return pltpu.make_async_remote_copy(
+            src_ref=data.at[pl.ds(0, size)], dst_ref=data.at[pl.ds(0, size)],
+            send_sem=send_sem.at[0], recv_sem=recv_sem.at[lane],
+            device_id=sibling, device_id_type=MESH,
+        )
 
     zed = my // 2
     spot = (mx // 2) * size_b + lax.rem(my, 2)
@@ -135,44 +120,104 @@
     peers = [(0, 0, step) for step in line[1:]] + [(p3, p2, 0) for p3, p2 in plane]
     peers.sort(key=lambda p: (p[0] > 0) + (p[1] > 0) + p[2])
 
+    cross = size_a == 2 and size_c <= SMALL
+    tie = lax.rem(mx // 2 + lax.rem(my, 2), 2) == 1
+
     def outer(peer):
-        return outer_line(peer[2]) if peer[2] else outer_plane(peer[0], peer[1])
-
-    def relay(kind, t):
-        p1 = t % size_c
+        if peer[2]:
+            return outer_line(peer[2])
+        return outer_plane(peer[0], peer[1])
+
+    def diagonal(peer):
+        return cross and peer[0] > 0 and peer[1] > 0
+
+    def within(peer):
+        inner = jnp.logical_not(outer(peer))
+        return jnp.logical_and(inner, jnp.logical_not(tie)) if diagonal(peer) else inner
+
+    def beyond(peer):
+        return jnp.logical_or(outer(peer), tie) if diagonal(peer) else outer(peer)
+
+    def greeted(peer):
+        return jnp.logical_and(outer(peer), jnp.logical_not(tie)) if diagonal(peer) else outer(peer)
+
+    def mark(peer):
+        return ready.at[peer[2] if max(peer[:2]) == 0 else size_c + plane.index((peer[0], peer[1]))]
+
+    def offer(peer):
+        return copy(0, label(*peer), at_step(*peer))
+
+    def spread(t):
+        return [copy(t, label(p3, p2, t), at_step(p3, p2, 0)) for p3, p2 in plane]
+
+    def hand_over(t):
+        return copy(t, t + half, sibling)
+
+    def relay(t):
         if 0 < t < size_c:
-            for p3, p2 in plane:
-                go = jnp.logical_not(inward(p3, p2, 0)) if hub else None
-                launch(kind, t, label(p3, p2, p1), at_step(p3, p2, 0), go)
+            for one in spread(t):
+                one.start()
         if t < half:
-            launch(kind, t, t + half, sibling)
-
-    def begin(kind):
-        if hub:
-            for p3, p2 in plane:
-                for step in line[1:]:
-                    launch(kind, 0, label(p3, p2, step), at_step(p3, p2, step), inward(p3, p2, step))
+            hand_over(t).start()
+
+    def arrive(t):
+        copy(0, t, sibling).wait_recv()
+        relay(t)
+
+    def answered(peer):
+        pl.semaphore_wait(mark(peer), 1)
+        offer(peer).start()
+
+    def answer(peer, device):
+        pl.semaphore_signal(mark(peer), inc=1, device_id=device, device_id_type=MESH)
+
+    def begin():
+        for k in line if size_c <= SMALL else []:
+
+            @pl.when(zed == k)
+            def _(k=k):
+                for target in range(k):
+                    offer((0, 0, k ^ target)).start()
+
         for peer in reversed(peers):
-            go = jnp.logical_not(outer(peer))
-            launch(kind, 0, label(*peer), at_step(*peer), go)
+            if peer[2] == 0 or size_c > SMALL:
+                pl.when(within(peer))(offer(peer).start)
 
         @pl.when(core == 0)
         def _():
             pl.semaphore_wait(ready.at[0], 1)
 
-        relay(kind, 0)
+        relay(0)
         for peer in peers:
-            go = outer(peer)
-
-            @pl.when(go)
-            def _(peer=peer):
-                pl.semaphore_wait(ready.at[label(*peer)], 1)
-
-            launch(kind, 0, label(*peer), at_step(*peer), go)
-
-    def arrive(kind, t):
-        copy(kind, 0, t, sibling).wait_recv()
-        relay(kind, t)
+            if (peer[2] == 0 and not diagonal(peer)) or size_c > SMALL:
+                pl.when(outer(peer))(functools.partial(answered, peer))
+        if cross:
+
+            @pl.when(spot == 0)
+            def _():
+                for peer in peers:
+                    if peer[2] == 0 and not diagonal(peer):
+                        answer((1, 1, 0), at_step(*peer))
+
+        if size_c > SMALL:
+            for t in line[1:]:
+                arrive(t)
+            return
+        for k in line:
+
+            @pl.when(zed == k)
+            def _(k=k):
+                near = sorted(line[1:], key=lambda t: (abs((k ^ t) - k), -(k ^ t)))
+                away = [(0, 0, t) for t in near if k ^ t > k]
+                for peer in away if k else away[:1]:
+                    answered(peer)
+                for peer in peers:
+                    if diagonal(peer):
+                        pl.when(beyond(peer))(functools.partial(answered, peer))
+                for t in near:
+                    if not k and t != near[0]:
+                        answered((0, 0, t))
+                    arrive(t)
 
     own = [
         pltpu.make_async_copy(pos, raw_pos, local_sem.at[0]),
@@ -187,34 +232,22 @@
     def greet(device):
         pl.semaphore_signal(barrier, inc=1, device_id=device, device_id_type=MESH)
 
-    def answer(t, device):
-        pl.semaphore_signal(ready.at[t], inc=1, device_id=device, device_id_type=MESH)
-
     for one in own:
         one.start()
     for peer in peers:
-        pl.when(outer(peer))(functools.partial(greet, at_step(*peer)))
+        pl.when(greeted(peer))(functools.partial(greet, at_step(*peer)))
     pl.when(core == 0)(functools.partial(greet, sibling))
-    extra = 0
-    if hub:
-
-        @pl.when(first)
-        def _():
-            for p3, p2 in plane:
-                for step in line[1:]:
-                    greet(at_step(p3, p2, step))
-
-        off = jnp.minimum(spot, 1)
-        extra = off * jnp.minimum(zed, 1)
-    lower = zed + spot + core + extra
+    lower = zed + spot + core
+    if cross:
+        lower = lower - jnp.where(spot == 2, 1, 0)
 
     @pl.when(lower > 0)
     def _():
         pl.semaphore_wait(barrier, lower)
 
     for peer in peers:
-        pl.when(jnp.logical_not(outer(peer)))(functools.partial(answer, label(*peer), at_step(*peer)))
-    pl.when(core == 1)(functools.partial(answer, 0, sibling))
+        pl.when(within(peer))(functools.partial(answer, peer, at_step(*peer)))
+    pl.when(core == 1)(functools.partial(answer, (0, 0, 0), sibling))
     for one in own:
         one.wait()
     mine = place_of[0]
@@ -230,7 +263,7 @@
     terms[...] = jnp.zeros_like(terms)
     state[0:3, :] = cen_out[...]
     state[3:4, :] = rad_out[...]
-    begin(1)
+    begin()
 
     lane0 = me * slots - row_me * 128
     lanes = lax.broadcasted_iota(jnp.int32, (GROUP, halo_dev), 1).astype(jnp.float32)
@@ -291,20 +324,20 @@
             oz = points[g, 2, at] - cz
             m = points[g, 3, at]
             u = jnp.sqrt(ox * ox + oy * oy + oz * oz) * scale
-            top = m * jnp.minimum(u + 0.5, 1.0)
-            ramp = m * (1.5 - u)
+            ramp = m * (0.5 - u)
             out = []
-            for k in range(SHELLS):
-                out.append(acc[k] + fold(jnp.maximum(jnp.minimum(top, ramp), 0.0)))
+            for k in range(SHELLS + 1):
+                out.append(acc[k] + fold(jnp.maximum(ramp, 0.0)))
                 ramp = ramp + m
             inner = m * jnp.clip(SHELLS / 2.0 - u, 0.0, 1.0)
-            out.append(acc[SHELLS] + fold(inner))
+            out.append(acc[SHELLS + 1] + fold(inner))
             for i, o in enumerate((ox, oy, oz)):
-                out.append(acc[SHELLS + 1 + i] + fold(o * inner))
+                out.append(acc[SHELLS + 2 + i] + fold(o * inner))
             return tuple(out)
 
         zero = jnp.zeros((8, width), jnp.float32)
-        acc = lax.fori_loop(0, BLOCK // CHUNK, chunk, (zero,) * (SHELLS + 4))
+        acc = lax.fori_loop(0, BLOCK // CHUNK, chunk, (zero,) * (SHELLS + 5))
+        acc = [acc[k + 1] - acc[k] - acc[0] for k in range(SHELLS)] + list(acc[SHELLS + 1 :])
         for k in range(SHELLS + 4):
             terms[k : k + 1, pl.ds(lo, width)] = jnp.sum(acc[k], axis=0, keepdims=True)
 
@@ -343,27 +376,15 @@
         state[0:3, :] = state[0:3, :] + sums[SHELLS + 1 : SHELLS + 4] / total
         return sums
 
-    split = kinds[0] is not None
-
-    def both(t):
-        if split:
-            arrive(0, t)
-        arrive(1, t)
-
-    if split:
-        for t in line[1:]:
-            arrive(0, t)
-    for t in line[1:]:
-        arrive(1, t)
     level = [rank[i][1] if rank[i][0] else -1 for i in range(n)]
     done = 0
     for p1 in line:
         for p3, p2 in reversed(plane):
-            both(label(p3, p2, p1))
+            arrive(label(p3, p2, p1))
         while done < groups and (p1 == line[-1] or level[(done + 1) * GROUP - 1] < p1):
-            for i in range(done * GROUP, (done + 1) * GROUP):
-                if rank[i][3] >= half:
-                    both(rank[i][3])
+            late = sum(rank[i][3] >= half for i in range(done * GROUP, (done + 1) * GROUP))
+            if late:
+                several(late, half - 1 + done).wait_recv()
             prepare(done)
             compute(done)
             done += 1
@@ -375,11 +396,7 @@
     cen_out[...] = state[0:3, :]
     rad_out[...] = state[3:4, :]
     prof_out[...] = sums[:SHELLS]
-    for one, go in sent:
-        if go is None:
-            one.wait_send()
-        else:
-            pl.when(go)(one.wait_send)
+    several(n - 1, 0).wait_send()
 
 
 def hand(a, b, c, x, y, z, sem):
@@ -427,9 +444,9 @@
             pltpu.VMEM((16, halo_dev), f32),
             pltpu.VMEM((16, total), f32),
             dma((6,)),
-            dma((2 * n,)),
-            dma((2 * n,)),
-            pltpu.SemaphoreType.REGULAR((n // 2,)),
+            dma((1,)),
+            dma((n // 2 - 1 + groups,)),
+            pltpu.SemaphoreType.REGULAR((ndx + ndy // 2,)),
         ],
         compiler_params=pltpu.CompilerParams(collective_id=0, has_side_effects=True),
     )(

time: 20.8 us -> 19.3 us (0.928)
  the two profiles are of different devices: /device:TPU:0 before, /device:TPU:17 now
where the time goes in v2:
time: 19.3 us; the launch traced here: 19.1 us
  Pallas kernels  18.4 us (95%)
  between operations  0.64 us (3%)
    pallas_call x1, Pallas kernels, body(): pl.pallas_call(functools.partial(kernel, (ndx, ndy, slots, count)), out_s...  17.8 us
    pallas_call x1, Pallas kernels, body(): pl.pallas_call(hand, out_shape=tuple((jax.ShapeDtypeStruct(x.shape, f32)...  0.67 us

profile of v2, /device:TPU:17, one launch (start us, length us, event | category | flops | bytes accessed | tf_op | source)
XLA Modules:
  0.0 19.1 jit_solution(2758050774618118532)
XLA Ops:
  0.6 17.8 %shard_map.85 = (f32[3,1024]{1,0:T(4,128)S(1)}, f32[1,1024]{1,0:T(1,128)S(1)}, f32[16,1024]{1,0:T(8,128)S(1)}) custom-call(f32[3,2048]{1,0:T(4,128)} %pos.1, f32[16,128]{1,0:T(8,128)} %bitcast.5, f32[3,1024]{1,0:T(4,128)} %cen.1, f32[1,1024]{1,0:T(1,128)} %bitcast.6, s32[4,128]{1,0:T(4,128)} %bitcast.7, s32[4,128]{1,0:T(4,128)} %bitcast.8), custom_call_target="tpu_custom_call" | custom-call | tf_op jit(solution)/shard_map/pallas_call | solution.py:426
  18.4 0.7 %shard_map.86 = (f32[3,1024]{1,0:T(4,128)}, f32[1,1024]{1,0:T(1,128)}, f32[16,1024]{1,0:T(8,128)}) custom-call(f32[3,1024]{1,0:T(4,128)S(1)} %get-tuple-element.9.a, f32[1,1024]{1,0:T(1,128)S(1)} %get-tuple-element.10.b, f32[16,1024]{1,0:T(8,128)S(1)} %get-tuple-element.11.c), custom_call_target="tpu_custom_call" | custom-call | tf_op jit(solution)/shard_map/pallas_call | solution.py:461

commit v3 on v2

--- a/solution.py
+++ b/solution.py
@@ -33,7 +33,7 @@
     sizes,
     pos, mass, cen, rad, blocks, halos,
     cen_out, rad_out, prof_out,
-    raw_pos, raw_mass, raw_pair, data, pick, points, onehot, terms, state, asked,
+    raw_pos, raw_mass, raw_pair, asking, data, pick, points, onehot, terms, state, asked,
     local_sem, send_sem, recv_sem, ready,
 ):
     ndx, ndy, slots, count = sizes
@@ -70,8 +70,10 @@
         return 2 * a + core, 2 * c + b
 
     sibling = (mx + 1 - 2 * core, my)
-    row_me = (me * slots) // 128
-    pair_rows = raw_pair.shape[1]
+    share = size_b * slots
+    asks = ndx * share // 128
+    body_rows = 4 * count
+    row_me = mx * share // 128
 
     def label(p3, p2, p1):
         return (p3 * size_b + p2) * size_c + p1
@@ -94,9 +96,22 @@
         return t - 1 if t < half else half - 1 + place_of[t] // GROUP
 
     def copy(source, target, device):
+        rows = body_rows if source == 0 and target < size_c else body_rows + 2 * asks
+        if source == target:
+            rows = body_rows + 2 * asks
         return pltpu.make_async_remote_copy(
-            src_ref=data.at[place_of[source]], dst_ref=data.at[place_of[target]],
+            src_ref=data.at[place_of[source], pl.ds(0, rows)],
+            dst_ref=data.at[place_of[target], pl.ds(0, rows)],
             send_sem=send_sem.at[0], recv_sem=recv_sem.at[lane_of(target)],
+            device_id=device, device_id_type=MESH,
+        )
+
+    def wanted(step, device):
+        slot = place_of[step]
+        return pltpu.make_async_remote_copy(
+            src_ref=asking.at[at_step(0, 0, step)[1] // 2],
+            dst_ref=data.at[slot, pl.ds(body_rows, 2 * asks)],
+            send_sem=send_sem.at[0], recv_sem=recv_sem.at[lane_of(step)],
             device_id=device, device_id_type=MESH,
         )
 
@@ -144,8 +159,19 @@
     def mark(peer):
         return ready.at[peer[2] if max(peer[:2]) == 0 else size_c + plane.index((peer[0], peer[1]))]
 
+    class Pair:
+        def __init__(self, *parts):
+            self.parts = parts
+
+        def start(self):
+            for part in self.parts:
+                part.start()
+
     def offer(peer):
-        return copy(0, label(*peer), at_step(*peer))
+        one = copy(0, label(*peer), at_step(*peer))
+        if peer[2]:
+            return Pair(one, wanted(peer[2], at_step(*peer)))
+        return one
 
     def spread(t):
         return [copy(t, label(p3, p2, t), at_step(p3, p2, 0)) for p3, p2 in plane]
@@ -155,13 +181,20 @@
 
     def relay(t):
         if 0 < t < size_c:
-            for one in spread(t):
-                one.start()
+            if cross:
+                corner, *sides = spread(t)
+                pl.when(spot == 3)(corner.start)
+                for one in sides:
+                    one.start()
+                pl.when(spot != 3)(corner.start)
+            else:
+                for one in spread(t):
+                    one.start()
         if t < half:
             hand_over(t).start()
 
     def arrive(t):
-        copy(0, t, sibling).wait_recv()
+        copy(t, t, sibling).wait_recv()
         relay(t)
 
     def answered(peer):
@@ -207,16 +240,14 @@
 
             @pl.when(zed == k)
             def _(k=k):
-                near = sorted(line[1:], key=lambda t: (abs((k ^ t) - k), -(k ^ t)))
+                near = sorted(line[1:], key=lambda t: (abs((k ^ t) - k), k ^ t))
                 away = [(0, 0, t) for t in near if k ^ t > k]
-                for peer in away if k else away[:1]:
+                for peer in away:
                     answered(peer)
                 for peer in peers:
                     if diagonal(peer):
                         pl.when(beyond(peer))(functools.partial(answered, peer))
                 for t in near:
-                    if not k and t != near[0]:
-                        answered((0, 0, t))
                     arrive(t)
 
     own = [
@@ -256,16 +287,29 @@
         for i in range(3):
             data[mine, i * count + b : i * count + b + 1, :] = part[i : i + 1]
     data[mine, 3 * count : 4 * count, :] = raw_mass[...]
+    groups_of = lax.broadcasted_iota(jnp.int32, (1, 128), 1) // share
     for i in range(2):
-        at = 4 * count + i * pair_rows
-        data[mine, at : at + pair_rows, :] = raw_pair[i].astype(jnp.float32)
+        values = raw_pair[i].astype(jnp.float32)
+        turned = {0: values}
+        for z in line:
+            for row in range(asks):
+                total = jnp.zeros((1, 128), jnp.float32)
+                for part in range(128 // share):
+                    start = ((row * (128 // share) + part) * size_c + z) * share
+                    turn = (part * share - start) % 128
+                    if turn not in turned:
+                        turned[turn] = pltpu.roll(values, turn, 1)
+                    piece = turned[turn][start // 128 : start // 128 + 1]
+                    total = jnp.where(groups_of == part, piece, total)
+                asking[z, i * asks + row : i * asks + row + 1, :] = total
+    data[mine, pl.ds(body_rows, 2 * asks), :] = asking[zed]
     state[...] = jnp.zeros_like(state)
     terms[...] = jnp.zeros_like(terms)
     state[0:3, :] = cen_out[...]
     state[3:4, :] = rad_out[...]
     begin()
 
-    lane0 = me * slots - row_me * 128
+    lane0 = lax.rem(mx * share, 128) + lax.rem(my, 2) * slots
     lanes = lax.broadcasted_iota(jnp.int32, (GROUP, halo_dev), 1).astype(jnp.float32)
     spots = lax.broadcasted_iota(jnp.int32, (GROUP, GROUP * count), 1).astype(jnp.float32)
     place = lax.broadcasted_iota(jnp.int32, (GROUP, 128), 0).astype(jnp.float32)
@@ -277,7 +321,7 @@
             lo = pl.multiple_of(lo, GROUP * slots)
 
         def taken(i):
-            at = 4 * count + i * pair_rows + row_me
+            at = body_rows + i * asks + row_me
             part = data[pl.ds(g * GROUP, GROUP), pl.ds(at, 1), :].reshape(GROUP, 128)
             return pltpu.roll(part, shift, 1)
 
@@ -376,18 +420,39 @@
         state[0:3, :] = state[0:3, :] + sums[SHELLS + 1 : SHELLS + 4] / total
         return sums
 
-    level = [rank[i][1] if rank[i][0] else -1 for i in range(n)]
-    done = 0
-    for p1 in line:
+    def plane_of(p1):
         for p3, p2 in reversed(plane):
             arrive(label(p3, p2, p1))
-        while done < groups and (p1 == line[-1] or level[(done + 1) * GROUP - 1] < p1):
-            late = sum(rank[i][3] >= half for i in range(done * GROUP, (done + 1) * GROUP))
-            if late:
-                several(late, half - 1 + done).wait_recv()
-            prepare(done)
-            compute(done)
-            done += 1
+
+    def finish(g):
+        late = sum(rank[i][3] >= half for i in range(g * GROUP, (g + 1) * GROUP))
+        if late:
+            several(late, half - 1 + g).wait_recv()
+        prepare(g)
+        compute(g)
+
+    def closer(k):
+        return sorted(line[1:], key=lambda t: (abs((k ^ t) - k), k ^ t))
+
+    plane_of(0)
+    finish(0)
+    if size_c <= SMALL:
+        for k in line:
+
+            @pl.when(zed == k)
+            def _(k=k):
+                for i, p1 in enumerate(closer(k)):
+                    plane_of(p1)
+                    if k == 0 and i == 0:
+                        finish(1)
+
+        pl.when(zed > 0)(functools.partial(finish, 1))
+    else:
+        for p1 in line[1:]:
+            plane_of(p1)
+        finish(1)
+    for g in range(2, groups):
+        finish(g)
     sums = advance()
     for step in range(1, ITERS):
         ask()
@@ -436,7 +501,8 @@
             pltpu.VMEM((3, count * BLOCK), f32),
             pltpu.VMEM((count, BLOCK), f32),
             pltpu.VMEM((2, total // 128, 128), jnp.int32),
-            pltpu.VMEM((n, 4 * count + 2 * (total // 128), BLOCK), f32),
+            pltpu.VMEM((ndy // 2, ndx * slots // 32, BLOCK), f32),
+            pltpu.VMEM((n, 4 * count + ndx * slots // 32, BLOCK), f32),
             pltpu.VMEM((total, GROUP * count), jnp.bfloat16),
             pltpu.VMEM((groups, 4, BLOCK, GROUP * slots), f32),
             pltpu.VMEM((total, halo_dev), jnp.bfloat16),

time: 19.3 us -> 18.1 us (0.938)
  the two profiles are of different devices: /device:TPU:17 before, /device:TPU:0 now
where the time goes in v3:
time: 18.1 us; the launch traced here: 17.9 us
  Pallas kernels  17.3 us (96%)
  between operations  0.64 us (4%)
    pallas_call x1, Pallas kernels, body(): pl.pallas_call(functools.partial(kernel, (ndx, ndy, slots, count)), out_s...  16.6 us
    pallas_call x1, Pallas kernels, body(): pl.pallas_call(hand, out_shape=tuple((jax.ShapeDtypeStruct(x.shape, f32)...  0.67 us

profile of v3, /device:TPU:0, one launch (start us, length us, event | category | flops | bytes accessed | tf_op | source)
XLA Modules:
  0.0 17.9 jit_solution(11222761002431988000)
XLA Ops:
  0.6 16.6 %shard_map.85 = (f32[3,1024]{1,0:T(4,128)S(1)}, f32[1,1024]{1,0:T(1,128)S(1)}, f32[16,1024]{1,0:T(8,128)S(1)}) custom-call(f32[3,2048]{1,0:T(4,128)} %pos.1, f32[16,128]{1,0:T(8,128)} %bitcast.5, f32[3,1024]{1,0:T(4,128)} %cen.1, f32[1,1024]{1,0:T(1,128)} %bitcast.6, s32[4,128]{1,0:T(4,128)} %bitcast.7, s32[4,128]{1,0:T(4,128)} %bitcast.8), custom_call_target="tpu_custom_call" | custom-call | tf_op jit(solution)/shard_map/pallas_call | solution.py:491
  17.3 0.7 %shard_map.86 = (f32[3,1024]{1,0:T(4,128)}, f32[1,1024]{1,0:T(1,128)}, f32[16,1024]{1,0:T(8,128)}) custom-call(f32[3,1024]{1,0:T(4,128)S(1)} %get-tuple-element.9.a, f32[1,1024]{1,0:T(1,128)S(1)} %get-tuple-element.10.b, f32[16,1024]{1,0:T(8,128)S(1)} %get-tuple-element.11.c), custom_call_target="tpu_custom_call" | custom-call | tf_op jit(solution)/shard_map/pallas_call | solution.py:527

commit v4 on v3

--- a/solution.py
+++ b/solution.py
@@ -9,7 +9,7 @@
 
 SHELLS = 16
 BLOCK = 128
-ITERS = 2
+KEEP = 24
 GROUP = 8
 ROWS = 32
 CHUNK = 32
@@ -33,7 +33,7 @@
     sizes,
     pos, mass, cen, rad, blocks, halos,
     cen_out, rad_out, prof_out,
-    raw_pos, raw_mass, raw_pair, asking, data, pick, points, onehot, terms, state, asked,
+    raw_pos, raw_mass, raw_pair, asking, data, pick, points, onehot, cols, same, terms, state, asked,
     local_sem, send_sem, recv_sem, ready,
 ):
     ndx, ndy, slots, count = sizes
@@ -307,6 +307,8 @@
     terms[...] = jnp.zeros_like(terms)
     state[0:3, :] = cen_out[...]
     state[3:4, :] = rad_out[...]
+    state[4:5, :] = lax.broadcasted_iota(jnp.int32, (1, halo_dev), 1).astype(jnp.float32)
+    state[5:6, :] = jnp.ones((1, halo_dev), jnp.float32)
     begin()
 
     lane0 = lax.rem(mx * share, 128) + lax.rem(my, 2) * slots
@@ -335,6 +337,9 @@
                 ]
                 both = jnp.concatenate(pair, axis=0).astype(jnp.bfloat16)
                 out[pl.ds(start, 2 * GROUP), :] = both
+            for i in (j, j + 1):
+                column = jnp.broadcast_to(rows[:, i : i + 1], (GROUP, GROUP * slots))
+                cols[pl.ds(lo + i * GROUP, GROUP), :] = column
         asked[:, pl.ds(lo, GROUP * slots)] = join3(
             lax.dot_general(
                 split3(state[...]), onehot[pl.ds(lo, GROUP * slots), :], (((1,), (1,)), ((), ())),
@@ -342,17 +347,25 @@
             )
         )
 
-    def ask():
-        asked[...] = join3(
-            lax.dot_general(
-                split3(state[...]), onehot[...], (((1,), (1,)), ((), ())),
-                preferred_element_type=jnp.float32,
-            )
-        )
+    def relate(g):
+        def block(h):
+            return pl.ds(h * width, width)
+
+        def meet(down, across):
+            key = asked[4:5, block(across)]
+            key = jnp.where(asked[5:6, block(across)] > 0.5, key, -2.0)
+            equal = cols[block(down), :] == key
+            same[block(down), block(across)] = jnp.where(equal, 1.0, 0.0).astype(jnp.bfloat16)
+
+        for h in range(g + 1):
+            meet(g, h)
+        for h in range(g):
+            meet(h, g)
 
     width = GROUP * slots
-
-    def evaluate(g):
+    kept = (SHELLS // 2 - 1, SHELLS, SHELLS + 1, SHELLS + 2, SHELLS + 3)
+
+    def evaluate(g, keep=False):
         lo = pl.multiple_of(g * width, width)
         mine = asked[0:4, pl.ds(lo, width)]
         cx, cy, cz, radius = (mine[i : i + 1] for i in range(4))
@@ -380,10 +393,14 @@
             return tuple(out)
 
         zero = jnp.zeros((8, width), jnp.float32)
-        acc = lax.fori_loop(0, BLOCK // CHUNK, chunk, (zero,) * (SHELLS + 5))
+        acc = lax.fori_loop(0, BLOCK // CHUNK, chunk, (zero,) * (SHELLS + 5), unroll=True)
         acc = [acc[k + 1] - acc[k] - acc[0] for k in range(SHELLS)] + list(acc[SHELLS + 1 :])
         for k in range(SHELLS + 4):
-            terms[k : k + 1, pl.ds(lo, width)] = jnp.sum(acc[k], axis=0, keepdims=True)
+            value = jnp.sum(acc[k], axis=0, keepdims=True)
+            terms[k : k + 1, pl.ds(lo, width)] = value
+            if keep and k in kept:
+                at = KEEP + kept.index(k)
+                terms[at : at + 1, pl.ds(lo, width)] = value
 
     def choose(g):
         chosen = pick[pl.ds(pl.multiple_of(g * width, width), width), :]
@@ -397,28 +414,28 @@
                 )
             )
 
-    def compute(g):
-        choose(g)
-        evaluate(g)
-
     def again(g, _):
         evaluate(g)
         return 0
 
-    def advance():
-        sums = join3(
+    def grown(radius, enclosed):
+        ratio = (1.0 + enclosed) / (1.0 + radius * radius * radius)
+        return radius * jnp.exp(jnp.log(ratio) * (1.0 / 3.0))
+
+    def gather_sums(values, table):
+        return join3(
             lax.dot_general(
-                split3(terms[...]), onehot[...], (((1,), (0,)), ((), ())),
+                split3(values), table, (((1,), (0,)), ((), ())),
                 preferred_element_type=jnp.float32,
             )
         )
-        radius = state[3:4, :]
-        enclosed = sums[SHELLS // 2 - 1 : SHELLS // 2]
-        ratio = (1.0 + enclosed) / (1.0 + radius * radius * radius)
-        state[3:4, :] = radius * jnp.exp(jnp.log(ratio) * (1.0 / 3.0))
-        total = jnp.maximum(sums[SHELLS : SHELLS + 1], 1.0)
-        state[0:3, :] = state[0:3, :] + sums[SHELLS + 1 : SHELLS + 4] / total
-        return sums
+
+    def move_slots():
+        part = gather_sums(terms[SHELLS : 2 * SHELLS], same[...])
+        enclosed = part[KEEP - SHELLS : KEEP - SHELLS + 1]
+        total = jnp.maximum(part[0:1], 1.0)
+        asked[3:4, :] = grown(asked[3:4, :], enclosed)
+        asked[0:3, :] = asked[0:3, :] + part[1:4] / total
 
     def plane_of(p1):
         for p3, p2 in reversed(plane):
@@ -429,7 +446,9 @@
         if late:
             several(late, half - 1 + g).wait_recv()
         prepare(g)
-        compute(g)
+        relate(g)
+        choose(g)
+        evaluate(g, True)
 
     def closer(k):
         return sorted(line[1:], key=lambda t: (abs((k ^ t) - k), k ^ t))
@@ -453,13 +472,19 @@
         finish(1)
     for g in range(2, groups):
         finish(g)
-    sums = advance()
-    for step in range(1, ITERS):
-        ask()
-        lax.fori_loop(0, groups, again, 0)
-        sums = advance()
-    cen_out[...] = state[0:3, :]
-    rad_out[...] = state[3:4, :]
+    move_slots()
+    lax.fori_loop(0, groups, again, 0)
+    sums = gather_sums(terms[...], onehot[...])
+    center, radius = state[0:3, :], state[3:4, :]
+    for first in (KEEP, None):
+        if first is None:
+            enclosed, inner = sums[SHELLS // 2 - 1 : SHELLS // 2], sums[SHELLS : SHELLS + 4]
+        else:
+            enclosed, inner = sums[first : first + 1], sums[first + 1 : first + 5]
+        radius = grown(radius, enclosed)
+        center = center + inner[1:4] / jnp.maximum(inner[0:1], 1.0)
+    cen_out[...] = center
+    rad_out[...] = radius
     prof_out[...] = sums[:SHELLS]
     several(n - 1, 0).wait_send()
 
@@ -506,6 +531,8 @@
             pltpu.VMEM((total, GROUP * count), jnp.bfloat16),
             pltpu.VMEM((groups, 4, BLOCK, GROUP * slots), f32),
             pltpu.VMEM((total, halo_dev), jnp.bfloat16),
+            pltpu.VMEM((total, GROUP * slots), f32),
+            pltpu.VMEM((total, total), jnp.bfloat16),
             pltpu.VMEM((ROWS, total), f32),
             pltpu.VMEM((16, halo_dev), f32),
             pltpu.VMEM((16, total), f32),

time: 18.1 us -> 17.3 us (0.956)
  Pallas kernels: 17.3 us -> 16.4 us
    pallas_call x1, Pallas kernels: 16.6 us -> 15.7 us  [body(): pl.pallas_call(functools.partial(kernel, (ndx, ndy, slots, count)), out_s...]
where the time goes in v4:
time: 17.3 us; the launch traced here: 17 us
  Pallas kernels  16.4 us (95%)
  between operations  0.64 us (4%)
    pallas_call x1, Pallas kernels, body(): pl.pallas_call(functools.partial(kernel, (ndx, ndy, slots, count)), out_s...  15.7 us
    pallas_call x1, Pallas kernels, body(): pl.pallas_call(hand, out_shape=tuple((jax.ShapeDtypeStruct(x.shape, f32)...  0.67 us

profile of v4, /device:TPU:0, one launch (start us, length us, event | category | flops | bytes accessed | tf_op | source)
XLA Modules:
  0.0 17.0 jit_solution(5968011042996690524)
XLA Ops:
  0.6 15.7 %shard_map.85 = (f32[3,1024]{1,0:T(4,128)S(1)}, f32[1,1024]{1,0:T(1,128)S(1)}, f32[16,1024]{1,0:T(8,128)S(1)}) custom-call(f32[3,2048]{1,0:T(4,128)} %pos.1, f32[16,128]{1,0:T(8,128)} %bitcast.5, f32[3,1024]{1,0:T(4,128)} %cen.1, f32[1,1024]{1,0:T(1,128)} %bitcast.6, s32[4,128]{1,0:T(4,128)} %bitcast.7, s32[4,128]{1,0:T(4,128)} %bitcast.8), custom_call_target="tpu_custom_call" | custom-call | tf_op jit(solution)/shard_map/pallas_call | solution.py:516
  16.4 0.7 %shard_map.86 = (f32[3,1024]{1,0:T(4,128)}, f32[1,1024]{1,0:T(1,128)}, f32[16,1024]{1,0:T(8,128)}) custom-call(f32[3,1024]{1,0:T(4,128)S(1)} %get-tuple-element.9.a, f32[1,1024]{1,0:T(1,128)S(1)} %get-tuple-element.10.b, f32[16,1024]{1,0:T(8,128)S(1)} %get-tuple-element.11.c), custom_call_target="tpu_custom_call" | custom-call | tf_op jit(solution)/shard_map/pallas_call | solution.py:554
